TPU v7x, 32 devices: a whole 2x2x4 slice. The times are simulated.
32 devices in a mesh: dp: 32 (over z, y, x, core), tensor: 1.
Axes of the slice: x: 2, y: 2, z: 4, core: 2. Of those that a mesh axis runs over, the one named last changes fastest.
Arguments:
- latent_raw: bfloat16 [6144, 512], P('dp'), may hold values from -6 to 6
- norm_gain: float32 [512], replicated, may hold values from 0.5 to 1.5
- up_weight: bfloat16 [512, 4096], P(None, 'tensor'), may hold values from -0.25 to 0.25
- grad_kv: bfloat16 [6144, 4096], P('dp', 'tensor'), may hold values from -3 to 3
Outputs:
- latent_grad: bfloat16 [6144, 512], P('dp')
- gain_grad: float32 [512], replicated
- weight_grad: float32 [512, 4096], P('dp', 'tensor')
All inputs are finite; a program needn't handle non-finite values.
Results may differ from a plain program's by a relative error of at most 0.0029.
Values may be sent and summed in bfloat16 or wider, within the bound.
A program may use at most 64 MiB of HBM per device.

v0:
```python
import functools

import jax
import jax.numpy as jnp
from jax import lax
from jax.experimental import pallas as pl
from jax.experimental.pallas import tpu as pltpu
from jax.sharding import PartitionSpec as P

epsilon = 1e-06
MESH = pl.DeviceIdType.MESH
CHUNKS = 4
LAG = 1
NORM_TURN = 1
GAIN_STEP = 1


def normalize(latent_raw):
    latent_full = latent_raw.astype(jnp.float32)
    inverse = lax.rsqrt(jnp.mean(latent_full * latent_full, axis=-1, keepdims=True) + epsilon)
    return (latent_full * inverse, inverse)


def norm_backward(grad_norm, scaled_rows, inverse, norm_gain):
    upstream = grad_norm * norm_gain
    centred = upstream - scaled_rows * jnp.mean(upstream * scaled_rows, axis=-1, keepdims=True)
    return (inverse * centred).astype(jnp.bfloat16)


def per_device(latent_raw, norm_gain, up_weight, grad_kv):
    scaled_rows, inverse = normalize(latent_raw)
    normed = (scaled_rows * norm_gain).astype(jnp.bfloat16)
    factor = float(latent_raw.shape[0] * lax.axis_size("dp")) ** (-0.5)
    partial_norm = lax.dot_general(
        grad_kv, up_weight, (((1,), (1,)), ((), ())), preferred_element_type=jnp.float32
    )
    grad_norm = lax.psum_scatter(partial_norm, "tensor", scatter_dimension=0, tiled=True)
    row_count = grad_norm.shape[0]
    offset = lax.axis_index("tensor") * row_count
    scaled_part = lax.dynamic_slice_in_dim(scaled_rows, offset, row_count, 0)
    inverse_part = lax.dynamic_slice_in_dim(inverse, offset, row_count, 0)
    gain_local = jnp.sum(grad_norm * scaled_part, axis=0)
    latent_part = norm_backward(grad_norm, scaled_part, inverse_part, norm_gain)
    latent_grad = lax.all_gather(latent_part, "tensor", axis=0, tiled=True)
    gain_grad = lax.psum(gain_local, ("dp", "tensor")) * factor
    weight_partial = lax.dot_general(
        normed, grad_kv, (((0,), (0,)), ((), ())), preferred_element_type=jnp.float32
    )
    weight_grad = lax.psum_scatter(weight_partial, "dp", scatter_dimension=0, tiled=True) * factor
    return (latent_grad, gain_grad, weight_grad)


def kernel(
    planes, factor, latent_hbm, gain_hbm, weight_hbm, grad_hbm,
    latent_out, gain_out, weight_out, latent_ref, gain_ref,
    own_grad, peer_grad, weight, turned, peer_turned, left,
    send_one, recv_one, keep_one, send_two, recv_two, keep_two,
    send_three, recv_three, keep_three, grad_norm, gain_send, gain_recv,
    small_sem, load_sem, weight_sem, turned_sem, grad_send_sem, grad_recv_sem,
    one_send_sem, one_recv_sem, two_send_sem, two_recv_sem,
    three_send_sem, three_recv_sem, gain_send_sem, gain_recv_sem,
):
    units, _, width = own_grad.shape
    chunks = units // 2
    rows = weight_out.shape[0]
    me = lax.axis_index("dp")
    core, x, y, z = me % 2, (me // 2) % 2, (me // 4) % 2, me // 8
    partner = me + 1 - 2 * core
    over_x = me + 2 - 4 * x
    over_y = me + 4 - 8 * y
    others = [(z + step) % planes for step in range(1, planes)]
    peers = [partner, over_x, over_y] + [other * 8 + me % 8 for other in others]

    def columns(unit):
        return pl.ds(unit * width, width)

    def send(source, target, send_sem, recv_sem, device):
        return pltpu.make_async_remote_copy(
            src_ref=source, dst_ref=target, send_sem=send_sem, recv_sem=recv_sem,
            device_id={"dp": device}, device_id_type=MESH,
        )

    small_loads = [
        pltpu.make_async_copy(latent_hbm, latent_ref, small_sem.at[0]),
        pltpu.make_async_copy(gain_hbm, gain_ref, small_sem.at[1]),
    ]
    for copy in small_loads:
        copy.start()
    order = [half * chunks + chunk for chunk in range(chunks) for half in range(2)]
    loads = {}
    for unit in order:
        loads[unit] = pltpu.make_async_copy(
            grad_hbm.at[:, columns(unit)], own_grad.at[unit], load_sem.at[unit]
        )
        loads[unit].start()
    weight_loads = {}
    for unit in order:
        weight_loads[unit] = pltpu.make_async_copy(
            weight_hbm.at[:, columns(unit)], weight.at[unit], weight_sem.at[unit]
        )
        weight_loads[unit].start()

    barrier = pltpu.get_barrier_semaphore()
    for peer in peers:
        pl.semaphore_signal(barrier, inc=1, device_id={"dp": peer}, device_id_type=MESH)

    for copy in small_loads:
        copy.wait()
    scaled_rows, _ = normalize(latent_ref[...])
    normed = scaled_rows * gain_ref[...]
    flipped = normed.T.astype(jnp.bfloat16)
    flipped = flipped.reshape(planes * 4, 2, rows, flipped.shape[1])
    turned[0] = flipped[:, 0]
    turned[1] = flipped[:, 1]

    pl.semaphore_wait(barrier, len(peers))

    grads = {}
    for position, unit in enumerate(order):
        loads[unit].wait()
        grads[unit] = send(
            own_grad.at[unit], peer_grad.at[unit],
            grad_send_sem.at[unit], grad_recv_sem.at[unit], partner,
        )
        grads[unit].start()
        if position == 0:
            turned_copy = send(
                turned.at[1 - core], peer_turned, turned_sem.at[0], turned_sem.at[1], partner
            )
            turned_copy.start()

    def block(plane, away_y, away_x):
        to_y = (1 - y) if away_y else y
        to_x = (1 - x) if away_x else x
        return plane * 4 + to_y * 2 + to_x

    def arrange(side, source):
        for first in range(2):
            for second in range(2):
                for plane in range(planes):
                    place = (first * 2 + second) * planes + plane
                    left[0, side, place] = source(block(plane, second == 0, first == 0))
                    left[1, side, place] = source(block(plane, first == 0, second == 0))

    arrange(0, lambda index: turned[core, index])
    turned_copy.wait_recv()
    arrange(1, lambda index: peer_turned[index])

    def left_of(half, side):
        value = left[half, side]
        return value.reshape(planes * 4 * rows, value.shape[-1])

    ones, twos, threes = {}, {}, {}
    half_rows = planes * 2 * rows
    quarter_rows = planes * rows

    def stage_one(unit):
        half = unit // chunks
        grads[unit].wait_recv()
        partial = jnp.dot(
            left_of(half, 0), own_grad[unit], preferred_element_type=jnp.float32
        ) + jnp.dot(left_of(half, 1), peer_grad[unit], preferred_element_type=jnp.float32)
        send_one[unit] = partial[:half_rows].astype(jnp.bfloat16)
        keep_one[unit] = partial[half_rows:]
        ones[unit] = send(
            send_one.at[unit], recv_one.at[unit],
            one_send_sem.at[unit], one_recv_sem.at[unit], over_y if half else over_x,
        )
        ones[unit].start()

    def stage_two(unit):
        half = unit // chunks
        ones[unit].wait_recv()
        total = keep_one[unit] + recv_one[unit].astype(jnp.float32)
        send_two[unit] = total[:quarter_rows].astype(jnp.bfloat16)
        keep_two[unit] = total[quarter_rows:]
        twos[unit] = send(
            send_two.at[unit], recv_two.at[unit],
            two_send_sem.at[unit], two_recv_sem.at[unit], over_x if half else over_y,
        )
        twos[unit].start()

    def stage_three(unit):
        twos[unit].wait_recv()
        total = keep_two[unit] + recv_two[unit].astype(jnp.float32)
        total = total.reshape(planes, rows, width)
        send_three[unit] = total.astype(jnp.bfloat16)
        keep_three[unit] = total
        for index, other in enumerate(others):
            threes[unit, index] = send(
                send_three.at[unit, other], recv_three.at[unit, z],
                three_send_sem.at[unit, other], three_recv_sem.at[unit, z], other * 8 + me % 8,
            )
            threes[unit, index].start()

    def arrival(unit, other):
        return send(
            send_three.at[unit, other], recv_three.at[unit, other],
            three_send_sem.at[unit, other], three_recv_sem.at[unit, other], other * 8 + me % 8,
        )

    def finish(unit):
        total = keep_three[unit, z]
        for other in others:
            arrival(unit, other).wait_recv()
            total = total + recv_three[unit, other].astype(jnp.float32)
        weight_out[:, columns(unit)] = total * factor

    def norm_part(unit, first):
        weight_loads[unit].wait()
        product = lax.dot_general(
            own_grad[unit], weight[unit], (((1,), (1,)), ((), ())),
            preferred_element_type=jnp.float32,
        )
        grad_norm[...] = product if first else grad_norm[...] + product

    gains = []

    def gain_send_to(stage, slot, device, at):
        copy = send(
            gain_send.at[stage], gain_recv.at[slot],
            gain_send_sem.at[at], gain_recv_sem.at[slot], device,
        )
        copy.start()
        gains.append(copy)

    def gain_pair(stage, device):
        gain_send_to(stage, stage, device, stage)

    def gain_take(stage):
        gains_of[stage].wait_recv()
        return gain_send[stage] + gain_recv[stage]

    gains_of = {}

    def gain_first(value):
        gain_send[0] = value
        gain_pair(0, partner)
        gains_of[0] = gains[-1]

    def gain_planes():
        value = gain_take(0)
        gain_send[3] = value
        gain_recv[3 + z] = value
        for index, other in enumerate(others):
            gain_send_to(3, 3 + z, other * 8 + me % 8, 3 + index)

    def gain_over_x():
        for index, other in enumerate(others):
            send(
                gain_send.at[3], gain_recv.at[3 + other],
                gain_send_sem.at[3 + index], gain_recv_sem.at[3 + other], other * 8 + me % 8,
            ).wait_recv()
        value = gain_recv[3]
        for plane in range(1, planes):
            value = value + gain_recv[3 + plane]
        gain_send[1] = value
        gain_pair(1, over_x)
        gains_of[1] = gains[-1]

    def gain_over_y():
        gain_send[2] = gain_take(1)
        gain_pair(2, over_y)
        gains_of[2] = gains[-1]

    def gain_end():
        gain_out[...] = gain_take(2) * factor

    def norm_rest():
        scaled, inverse = normalize(latent_ref[...])
        grads_here = grad_norm[...]
        gain_first(jnp.sum(grads_here * scaled, axis=0, keepdims=True))
        latent_out[...] = norm_backward(grads_here, scaled, inverse, gain_ref[...])

    def both(stage, chunk):
        if 0 <= chunk < chunks:
            stage(chunk)
            stage(chunks + chunk)

    for turn in range(chunks + 3 * LAG):
        both(stage_one, turn)
        if turn == NORM_TURN:
            for position, unit in enumerate(order):
                norm_part(unit, position == 0)
            norm_rest()
        both(stage_two, turn - LAG)
        if turn == NORM_TURN:
            gain_planes()
        both(stage_three, turn - 2 * LAG)
        if turn == NORM_TURN + GAIN_STEP:
            gain_over_x()
        if turn == NORM_TURN + 2 * GAIN_STEP:
            gain_over_y()
        if turn == NORM_TURN + 3 * GAIN_STEP:
            gain_end()
        both(finish, turn - 3 * LAG)

    turned_copy.wait_send()
    for group in (grads, ones, twos, threes):
        for copy in group.values():
            copy.wait_send()
    for copy in gains:
        copy.wait_send()


def place_kernel(first_in, second_in, third_in, first_out, second_out, third_out, sem):
    pairs = ((first_in, first_out), (second_in, second_out), (third_in, third_out))
    copies = [pltpu.make_async_copy(*pair, sem.at[at]) for at, pair in enumerate(pairs)]
    for copy in copies:
        copy.start()
    for copy in copies:
        copy.wait()


def place(*arrays):
    hbm = pl.BlockSpec(memory_space=pl.ANY)
    vmem = pl.BlockSpec(memory_space=pltpu.VMEM)
    return pl.pallas_call(
        place_kernel,
        out_shape=tuple(jax.ShapeDtypeStruct(a.shape, a.dtype) for a in arrays),
        in_specs=[vmem] * 3,
        out_specs=(hbm,) * 3,
        scratch_shapes=[pltpu.SemaphoreType.DMA((3,))],
        compiler_params=pltpu.CompilerParams(vmem_limit_bytes=8 * 1024 * 1024),
    )(*arrays)


def fused(latent_raw, norm_gain, up_weight, grad_kv):
    devices = lax.axis_size("dp")
    planes = devices // 8
    tokens, latent_width = latent_raw.shape
    total_columns = grad_kv.shape[1]
    units = 2 * CHUNKS
    width = total_columns // units
    rows = latent_width // devices
    factor = float(tokens * devices) ** (-0.5)
    half_rows, quarter_rows = planes * 2 * rows, planes * rows
    bf16, f32 = jnp.bfloat16, jnp.float32
    dma = pltpu.SemaphoreType.DMA
    vmem = pl.BlockSpec(memory_space=pltpu.VMEM)
    hbm = pl.BlockSpec(memory_space=pl.ANY)
    latent_grad, gain_grad, weight_grad = pl.pallas_call(
        functools.partial(kernel, planes, factor),
        out_shape=(
            pltpu.VMEM((tokens, latent_width), bf16),
            pltpu.VMEM((1, latent_width), f32),
            pltpu.VMEM((rows, total_columns), f32),
        ),
        in_specs=[pl.BlockSpec(memory_space=pltpu.HBM)] * 4,
        out_specs=(vmem, vmem, vmem),
        scratch_shapes=[
            pltpu.VMEM((tokens, latent_width), bf16),
            pltpu.VMEM((1, latent_width), f32),
            pltpu.VMEM((units, tokens, width), bf16),
            pltpu.VMEM((units, tokens, width), bf16),
            pltpu.VMEM((units, latent_width, width), bf16),
            pltpu.VMEM((2, planes * 4, rows, tokens), bf16),
            pltpu.VMEM((planes * 4, rows, tokens), bf16),
            pltpu.VMEM((2, 2, planes * 4, rows, tokens), bf16),
            pltpu.VMEM((units, half_rows, width), bf16),
            pltpu.VMEM((units, half_rows, width), bf16),
            pltpu.VMEM((units, half_rows, width), f32),
            pltpu.VMEM((units, quarter_rows, width), bf16),
            pltpu.VMEM((units, quarter_rows, width), bf16),
            pltpu.VMEM((units, quarter_rows, width), f32),
            pltpu.VMEM((units, planes, rows, width), bf16),
            pltpu.VMEM((units, planes, rows, width), bf16),
            pltpu.VMEM((units, planes, rows, width), f32),
            pltpu.VMEM((tokens, latent_width), f32),
            pltpu.VMEM((4, 1, latent_width), f32),
            pltpu.VMEM((3 + planes, 1, latent_width), f32),
            dma((2,)), dma((units,)), dma((units,)), dma((2,)), dma((units,)), dma((units,)),
            dma((units,)), dma((units,)), dma((units,)), dma((units,)),
            dma((units, planes)), dma((units, planes)),
            dma((3 + planes,)), dma((3 + planes,)),
        ],
        compiler_params=pltpu.CompilerParams(
            collective_id=0, has_side_effects=True, vmem_limit_bytes=67043328 - 512 * 1024
        ),
    )(latent_raw, norm_gain.reshape(1, latent_width), up_weight, grad_kv)
    latent_grad, gain_grad, weight_grad = place(latent_grad, gain_grad, weight_grad)
    return (latent_grad, gain_grad.reshape(latent_width), weight_grad)


def solution(mesh):
    devices = mesh.shape["dp"]
    covered = mesh.shape["tensor"] == 1 and devices % 8 == 0 and 16 <= devices <= 32
    in_specs = (P("dp", None), P(), P(None, "tensor"), P("dp", "tensor"))
    out_specs = (P("dp", None), P(), P("dp", "tensor"))
    return jax.shard_map(
        fused if covered else per_device,
        mesh=mesh, in_specs=in_specs, out_specs=out_specs, check_vma=False,
    )
```

profile of v0, /device:TPU:0, one launch (start us, length us, event | category | flops | bytes accessed | tf_op | source)
XLA Modules:
  0.0 35.9 jit_solution(9630876378333705689)
XLA Ops:
  0.6 34.4 %shard_map.67 = (bf16[192,512]{1,0:T(8,128)(2,1)S(1)}, f32[1,512]{1,0:T(1,128)S(1)}, f32[16,4096]{1,0:T(8,128)S(1)}) custom-call(bf16[192,512]{1,0:T(8,128)(2,1)} %latent_hbm.1, f32[1,512]{1,0:T(1,128)} %bitcast.2, bf16[512,4096]{1,0:T(8,128)(2,1)} %weight_hbm.1, bf16[192,4096]{1,0:T(8,128)(2,1)} %grad_hbm.1), custom_call_target="tpu_custom_call" | custom-call | tf_op jit(solution)/shard_map/pallas_call | solution.py:342
  35.1 0.8 %shard_map.68 = (bf16[192,512]{1,0:T(8,128)(2,1)}, f32[1,512]{1,0:T(1,128)}, f32[16,4096]{1,0:T(8,128)}) custom-call(bf16[192,512]{1,0:T(8,128)(2,1)S(1)} %get-tuple-element.9.first_in, f32[1,512]{1,0:T(1,128)S(1)} %get-tuple-element.10.second_in, f32[16,4096]{1,0:T(8,128)S(1)} %get-tuple-element.11.third_in), custom_call_target="tpu_custom_call" | custom-call | tf_op jit(solution)/shard_map/pallas_call | solution.py:318
where the time goes:
time: 36 us; the launch traced here: 35.9 us
  Pallas kernels  35.2 us (98%)
  between operations  0.64 us (2%)
    pallas_call x1, Pallas kernels, fused(): pl.pallas_call(functools.partial(kernel, planes, factor), out_shape=(pltp...  34.4 us
    pallas_call x1, Pallas kernels, place(): pl.pallas_call(place_kernel, out_shape=tuple((jax.ShapeDtypeStruct(a.shap...  0.8 us

commit v1 on v0

v1 whole, which is shorter than its diff:
```python
import functools

import jax
import jax.numpy as jnp
from jax import lax
from jax.experimental import pallas as pl
from jax.experimental.pallas import tpu as pltpu
from jax.sharding import PartitionSpec as P

epsilon = 1e-06
MESH = pl.DeviceIdType.MESH
FIRST_Z = (2, 4)
PAIRS = (2, 3, 2, 2, 2, 2)
GRANULES = 32
SEND, PASS, SPREAD, FINISH, NORM, GAIN = range(6)
NORMS = 3
ORDER = (
    (SEND, 0), (SEND, 2), (SEND, 3), (SEND, 1), (SEND, 4), (SEND, 5),
    (SEND, 6), (SEND, 7), (SEND, 8), (PASS, 2), (PASS, 3), (NORM, 0),
    (NORM, 1), (SEND, 9), (SEND, 10), (NORM, 2), (SEND, 11), (SEND, 12),
    (PASS, 4), (PASS, 5), (PASS, 0), (PASS, 6), (PASS, 7), (SPREAD, 2),
    (PASS, 8), (GAIN, 0), (SPREAD, 3), (PASS, 9), (SEND, 13), (PASS, 10),
    (PASS, 11), (PASS, 1), (SPREAD, 4), (PASS, 12), (FINISH, 2), (SPREAD, 6),
    (FINISH, 3), (SPREAD, 5), (SPREAD, 8), (FINISH, 0), (SPREAD, 7), (GAIN, 1),
    (SPREAD, 9), (PASS, 13), (FINISH, 4), (SPREAD, 11), (SPREAD, 10), (FINISH, 6),
    (FINISH, 1), (SPREAD, 12), (SPREAD, 13), (FINISH, 5), (FINISH, 8), (FINISH, 7),
    (FINISH, 9), (FINISH, 11), (GAIN, 2), (FINISH, 10), (FINISH, 12), (FINISH, 13),
)


def normalize(latent_raw):
    latent_full = latent_raw.astype(jnp.float32)
    inverse = lax.rsqrt(jnp.mean(latent_full * latent_full, axis=-1, keepdims=True) + epsilon)
    return (latent_full * inverse, inverse)


def norm_backward(grad_norm, scaled_rows, inverse, norm_gain):
    upstream = grad_norm * norm_gain
    centred = upstream - scaled_rows * jnp.mean(upstream * scaled_rows, axis=-1, keepdims=True)
    return (inverse * centred).astype(jnp.bfloat16)


def per_device(latent_raw, norm_gain, up_weight, grad_kv):
    scaled_rows, inverse = normalize(latent_raw)
    normed = (scaled_rows * norm_gain).astype(jnp.bfloat16)
    factor = float(latent_raw.shape[0] * lax.axis_size("dp")) ** (-0.5)
    partial_norm = lax.dot_general(
        grad_kv, up_weight, (((1,), (1,)), ((), ())), preferred_element_type=jnp.float32
    )
    grad_norm = lax.psum_scatter(partial_norm, "tensor", scatter_dimension=0, tiled=True)
    row_count = grad_norm.shape[0]
    offset = lax.axis_index("tensor") * row_count
    scaled_part = lax.dynamic_slice_in_dim(scaled_rows, offset, row_count, 0)
    inverse_part = lax.dynamic_slice_in_dim(inverse, offset, row_count, 0)
    gain_local = jnp.sum(grad_norm * scaled_part, axis=0)
    latent_part = norm_backward(grad_norm, scaled_part, inverse_part, norm_gain)
    latent_grad = lax.all_gather(latent_part, "tensor", axis=0, tiled=True)
    gain_grad = lax.psum(gain_local, ("dp", "tensor")) * factor
    weight_partial = lax.dot_general(
        normed, grad_kv, (((0,), (0,)), ((), ())), preferred_element_type=jnp.float32
    )
    weight_grad = lax.psum_scatter(weight_partial, "dp", scatter_dimension=0, tiled=True) * factor
    return (latent_grad, gain_grad, weight_grad)


def unit_list():
    units, start = [], 0
    for width in FIRST_Z:
        units.append(("z", start, width))
        start += width
    for width in PAIRS:
        for kind in ("x", "y"):
            units.append((kind, start, width))
            start += width
    return units


UNITS = unit_list()


def buffers(planes, kind, tokens, rows, width):
    bf16, f32 = jnp.bfloat16, jnp.float32
    shapes = [((tokens, width), bf16), ((tokens, width), bf16)]
    if kind == "z":
        shapes += [
            ((planes - 1, 4 * rows, width), bf16), ((planes - 1, 4 * rows, width), bf16),
            ((4 * rows, width), f32),
            ((3, rows, width), bf16), ((3, rows, width), bf16), ((rows, width), f32),
        ]
    else:
        half, quarter = 2 * planes * rows, planes * rows
        shapes += [
            ((half, width), bf16), ((half, width), bf16), ((half, width), f32),
            ((quarter, width), bf16), ((quarter, width), bf16), ((quarter, width), f32),
            ((planes - 1, rows, width), bf16), ((planes - 1, rows, width), bf16),
            ((rows, width), f32),
        ]
    return [pltpu.VMEM(shape, dtype) for shape, dtype in shapes]


def kernel(planes, factor, granule, *refs):
    refs = list(refs)

    def take(count):
        taken = refs[:count]
        del refs[:count]
        return taken

    latent_hbm, gain_hbm, weight_hbm, grad_hbm = take(4)
    latent_out, gain_out, weight_out = take(3)
    latent_ref, gain_ref, weight, turned, peer_turned, left = take(6)
    grad_norm, gain_send, gain_pair, gain_quad, gain_line = take(5)
    held = [take(8 if kind == "z" else 11) for kind, _, _ in UNITS]
    small_sem, local_sem, grad_sem, one_sem, two_sem, three_sem, gain_sem = take(7)

    rows = weight_out.shape[0]
    me = lax.axis_index("dp")
    core, x, y, z = me % 2, (me // 2) % 2, (me // 4) % 2, me // 8
    partner = me + 1 - 2 * core
    over_x = me + 2 - 4 * x
    over_y = me + 4 - 8 * y
    over_xy = over_x + 4 - 8 * y
    lines = [((z + step) % planes) * 8 + me % 8 for step in range(1, planes)]
    quad = [over_x, over_y, over_xy]
    peers = [partner] + quad + lines

    def columns(unit):
        _, start, width = UNITS[unit]
        return pl.ds(start * granule, width * granule)

    def send(source, target, send_sem, recv_sem, device):
        return pltpu.make_async_remote_copy(
            src_ref=source, dst_ref=target, send_sem=send_sem, recv_sem=recv_sem,
            device_id={"dp": device}, device_id_type=MESH,
        )

    small_loads = [
        pltpu.make_async_copy(latent_hbm, latent_ref, small_sem.at[0]),
        pltpu.make_async_copy(gain_hbm, gain_ref, small_sem.at[1]),
    ]
    for copy in small_loads:
        copy.start()
    firsts = [unit for stage, unit in ORDER if stage == SEND]
    loads = {}
    for unit in firsts:
        loads[unit] = pltpu.make_async_copy(
            grad_hbm.at[:, columns(unit)], held[unit][0], local_sem.at[unit]
        )
        loads[unit].start()

    barrier = pltpu.get_barrier_semaphore()
    for peer in peers:
        pl.semaphore_signal(barrier, inc=1, device_id={"dp": peer}, device_id_type=MESH)

    for copy in small_loads:
        copy.wait()
    scaled_rows, _ = normalize(latent_ref[...])
    normed = scaled_rows * gain_ref[...]
    flipped = normed.T.astype(jnp.bfloat16)
    flipped = flipped.reshape(planes * 4, 2, rows, flipped.shape[1])
    turned[0] = flipped[:, 0]
    turned[1] = flipped[:, 1]

    pl.semaphore_wait(barrier, len(peers))

    turned_copy = send(
        turned.at[1 - core], peer_turned, small_sem.at[0], small_sem.at[2], partner
    )
    turned_copy.start()
    grads = {}

    def share_grads(units):
        for unit in units:
            loads[unit].wait()
            grads[unit] = send(
                held[unit][0], held[unit][1], local_sem.at[unit], grad_sem.at[unit], partner
            )
            grads[unit].start()

    share_grads(firsts[:1])
    weight_load = pltpu.make_async_copy(weight_hbm, weight, small_sem.at[1])

    def block(step, away_y, away_x):
        to_y = (1 - y) if away_y else y
        to_x = (1 - x) if away_x else x
        return ((z + step) % planes) * 4 + to_y * 2 + to_x

    def arrange(kind, side, source):
        for step in range(planes):
            for first in range(2):
                for second in range(2):
                    if kind == "z":
                        place = step * 4 + first * 2 + second
                        left[0, side, place] = source(block(step, first, second))
                    else:
                        place = (first * 2 + second) * planes + step
                        if kind == "x":
                            index = block(step, second == 0, first == 0)
                        else:
                            index = block(step, first == 0, second == 0)
                        left[1 if kind == "x" else 2, side, place] = source(index)

    arrange("z", 0, lambda index: turned[core, index])
    share_grads(firsts[1:3])
    for kind in ("x", "y"):
        arrange(kind, 0, lambda index: turned[core, index])
    share_grads(firsts[3:])
    weight_load.start()
    turned_copy.wait_recv()
    arranged = set()

    half_rows = planes * 2 * rows
    quarter_rows = planes * rows
    local, ones, twos, threes = dict(grads), {}, {}, {}

    def partial_of(unit):
        kind = UNITS[unit][0]
        if kind not in arranged:
            arrange(kind, 1, lambda index: peer_turned[index])
            arranged.add(kind)
        which = ("z", "x", "y").index(kind)
        sides = [
            left[which, side].reshape(planes * 4 * rows, left.shape[-1]) for side in range(2)
        ]
        grads[unit].wait_recv()
        return jnp.dot(
            sides[0], held[unit][0][...], preferred_element_type=jnp.float32
        ) + jnp.dot(sides[1], held[unit][1][...], preferred_element_type=jnp.float32)

    def along_z(unit, source, target, recv_sem):
        for step, device in enumerate(lines):
            send(
                source.at[step], target.at[step], local_sem.at[unit], recv_sem, device
            ).start()
        return send(source, target, local_sem.at[unit], recv_sem, lines[0])

    def stage_send(unit):
        kind = UNITS[unit][0]
        partial = partial_of(unit)
        local[unit].wait_send()
        if kind == "z":
            outgoing, incoming, keep = held[unit][2:5]
            split = partial.reshape(planes, 4 * rows, partial.shape[1])
            outgoing[...] = split[1:].astype(jnp.bfloat16)
            keep[...] = split[0]
            local[unit] = ones[unit] = along_z(unit, outgoing, incoming, one_sem.at[unit])
        else:
            outgoing, incoming, keep = held[unit][2:5]
            outgoing[...] = partial[:half_rows].astype(jnp.bfloat16)
            keep[...] = partial[half_rows:]
            local[unit] = ones[unit] = send(
                outgoing, incoming, local_sem.at[unit], one_sem.at[unit],
                over_x if kind == "x" else over_y,
            )
            ones[unit].start()

    def stage_pass(unit):
        kind = UNITS[unit][0]
        ones[unit].wait_recv()
        local[unit].wait_send()
        incoming, keep = held[unit][3:5]
        total = keep[...]
        if kind == "z":
            for step in range(planes - 1):
                total = total + incoming[step].astype(jnp.float32)
            outgoing, landing, rest = held[unit][5:8]
            total = total.reshape(4, rows, total.shape[1])
            outgoing[...] = total[1:].astype(jnp.bfloat16)
            rest[...] = total[0]
            for slot, device in ((2, over_xy), (0, over_x), (1, over_y)):
                send(
                    outgoing.at[slot], landing.at[slot], local_sem.at[unit],
                    three_sem.at[unit], device,
                ).start()
            local[unit] = threes[unit] = send(
                outgoing, landing, local_sem.at[unit], three_sem.at[unit], over_x
            )
        else:
            total = total + incoming[...].astype(jnp.float32)
            outgoing, landing, rest = held[unit][5:8]
            outgoing[...] = total[:quarter_rows].astype(jnp.bfloat16)
            rest[...] = total[quarter_rows:]
            local[unit] = twos[unit] = send(
                outgoing, landing, local_sem.at[unit], two_sem.at[unit],
                over_y if kind == "x" else over_x,
            )
            twos[unit].start()

    def stage_spread(unit):
        twos[unit].wait_recv()
        local[unit].wait_send()
        landing, keep, outgoing, incoming, rest = held[unit][6:11]
        total = keep[...] + landing[...].astype(jnp.float32)
        total = total.reshape(planes, rows, total.shape[1])
        outgoing[...] = total[1:].astype(jnp.bfloat16)
        rest[...] = total[0]
        local[unit] = threes[unit] = along_z(unit, outgoing, incoming, three_sem.at[unit])

    def stage_finish(unit):
        threes[unit].wait_recv()
        incoming, keep = held[unit][-2:]
        total = keep[...]
        for index in range(incoming.shape[0]):
            total = total + incoming[index].astype(jnp.float32)
        weight_out[:, columns(unit)] = total * factor

    gains = {}

    def gain_start(stage, copies, whole):
        for copy in copies:
            copy.start()
        gains[stage] = whole

    def norm_piece(piece):
        if piece == 0:
            weight_load.wait()
        share = -(-len(firsts) // NORMS)
        total = None if piece == 0 else grad_norm[...]
        for unit in firsts[piece * share : (piece + 1) * share]:
            product = lax.dot_general(
                held[unit][0][...], weight[:, columns(unit)], (((1,), (1,)), ((), ())),
                preferred_element_type=jnp.float32,
            )
            total = product if total is None else total + product
        grad_norm[...] = total
        if piece == NORMS - 1:
            scaled, inverse = normalize(latent_ref[...])
            gain_send[0] = jnp.sum(total * scaled, axis=0, keepdims=True)
            copy = send(gain_send.at[0], gain_pair, gain_sem.at[0], gain_sem.at[1], partner)
            gain_start(0, [copy], copy)
            latent_out[...] = norm_backward(total, scaled, inverse, gain_ref[...])

    def gain_step(stage):
        gains[stage].wait_recv()
        gains[stage].wait_send()
        if stage == 0:
            gain_send[1] = gain_send[0] + gain_pair[...]
            copies = [
                send(gain_send.at[1], gain_quad.at[slot], gain_sem.at[0], gain_sem.at[2], device)
                for slot, device in enumerate(quad)
            ]
            whole = send(gain_quad, gain_quad, gain_sem.at[0], gain_sem.at[2], over_x)
            gain_start(1, copies, whole)
        elif stage == 1:
            value = (gain_send[1] + gain_quad[0]) + (gain_quad[1] + gain_quad[2])
            gain_send[2] = value
            gain_line[0] = value
            copies = [
                send(
                    gain_send.at[2], gain_line.at[step + 1],
                    gain_sem.at[0], gain_sem.at[3], device,
                )
                for step, device in enumerate(lines)
            ]
            landed = gain_line.at[pl.ds(1, planes - 1)]
            gain_start(2, copies, send(landed, landed, gain_sem.at[0], gain_sem.at[3], lines[0]))
        else:
            value = gain_line[z % planes]
            for plane in range(1, planes):
                value = value + gain_line[(z - plane + planes) % planes]
            gain_out[...] = value * factor

    stages = (stage_send, stage_pass, stage_spread, stage_finish, norm_piece, gain_step)
    for stage, unit in ORDER:
        stages[stage](unit)

    turned_copy.wait_send()
    for copy in local.values():
        copy.wait_send()


def place_kernel(first_in, second_in, third_in, first_out, second_out, third_out, sem):
    pairs = ((first_in, first_out), (second_in, second_out), (third_in, third_out))
    copies = [pltpu.make_async_copy(*pair, sem.at[at]) for at, pair in enumerate(pairs)]
    for copy in copies:
        copy.start()
    for copy in copies:
        copy.wait()


def place(*arrays):
    hbm = pl.BlockSpec(memory_space=pl.ANY)
    vmem = pl.BlockSpec(memory_space=pltpu.VMEM)
    return pl.pallas_call(
        place_kernel,
        out_shape=tuple(jax.ShapeDtypeStruct(a.shape, a.dtype) for a in arrays),
        in_specs=[vmem] * 3,
        out_specs=(hbm,) * 3,
        scratch_shapes=[pltpu.SemaphoreType.DMA((3,))],
        compiler_params=pltpu.CompilerParams(vmem_limit_bytes=8 * 1024 * 1024),
    )(*arrays)


def fused(latent_raw, norm_gain, up_weight, grad_kv):
    devices = lax.axis_size("dp")
    planes = devices // 8
    tokens, latent_width = latent_raw.shape
    total_columns = grad_kv.shape[1]
    granule = total_columns // GRANULES
    rows = latent_width // devices
    factor = float(tokens * devices) ** (-0.5)
    bf16, f32 = jnp.bfloat16, jnp.float32
    dma = pltpu.SemaphoreType.DMA
    vmem = pl.BlockSpec(memory_space=pltpu.VMEM)
    count = len(UNITS)
    held = []
    for kind, _, width in UNITS:
        held += buffers(planes, kind, tokens, rows, width * granule)
    latent_grad, gain_grad, weight_grad = pl.pallas_call(
        functools.partial(kernel, planes, factor, granule),
        out_shape=(
            pltpu.VMEM((tokens, latent_width), bf16),
            pltpu.VMEM((1, latent_width), f32),
            pltpu.VMEM((rows, total_columns), f32),
        ),
        in_specs=[pl.BlockSpec(memory_space=pltpu.HBM)] * 4,
        out_specs=(vmem, vmem, vmem),
        scratch_shapes=[
            pltpu.VMEM((tokens, latent_width), bf16),
            pltpu.VMEM((1, latent_width), f32),
            pltpu.VMEM((latent_width, total_columns), bf16),
            pltpu.VMEM((2, planes * 4, rows, tokens), bf16),
            pltpu.VMEM((planes * 4, rows, tokens), bf16),
            pltpu.VMEM((3, 2, planes * 4, rows, tokens), bf16),
            pltpu.VMEM((tokens, latent_width), f32),
            pltpu.VMEM((3, 1, latent_width), f32),
            pltpu.VMEM((1, latent_width), f32),
            pltpu.VMEM((3, 1, latent_width), f32),
            pltpu.VMEM((planes, 1, latent_width), f32),
            *held,
            dma((3,)), dma((count,)), dma((count,)), dma((count,)),
            dma((count,)), dma((count,)), dma((4,)),
        ],
        compiler_params=pltpu.CompilerParams(
            collective_id=0, has_side_effects=True, vmem_limit_bytes=67043328 - 512 * 1024
        ),
    )(latent_raw, norm_gain.reshape(1, latent_width), up_weight, grad_kv)
    latent_grad, gain_grad, weight_grad = place(latent_grad, gain_grad, weight_grad)
    return (latent_grad, gain_grad.reshape(latent_width), weight_grad)


def solution(mesh):
    devices = mesh.shape["dp"]
    covered = mesh.shape["tensor"] == 1 and devices % 8 == 0 and 16 <= devices <= 32
    in_specs = (P("dp", None), P(), P(None, "tensor"), P("dp", "tensor"))
    out_specs = (P("dp", None), P(), P("dp", "tensor"))
    return jax.shard_map(
        fused if covered else per_device,
        mesh=mesh, in_specs=in_specs, out_specs=out_specs, check_vma=False,
    )
```

time: 36 us -> 31.6 us (0.88)
  Pallas kernels: 35.2 us -> 30.8 us
    pallas_call x1, Pallas kernels: 34.4 us -> 30 us  [fused(): pl.pallas_call(functools.partial(kernel, planes, factor, granule), out_sh...]
where the time goes in v1:
time: 31.6 us; the launch traced here: 31.5 us
  Pallas kernels  30.8 us (97%)
  between operations  0.64 us (2%)
    pallas_call x1, Pallas kernels, fused(): pl.pallas_call(functools.partial(kernel, planes, factor, granule), out_sh...  30 us
    pallas_call x1, Pallas kernels, place(): pl.pallas_call(place_kernel, out_shape=tuple((jax.ShapeDtypeStruct(a.shap...  0.8 us

profile of v1, /device:TPU:0, one launch (start us, length us, event | category | flops | bytes accessed | tf_op | source)
XLA Modules:
  0.0 31.5 jit_solution(13924033667863521235)
XLA Ops:
  0.6 30.0 %shard_map.67 = (bf16[192,512]{1,0:T(8,128)(2,1)S(1)}, f32[1,512]{1,0:T(1,128)S(1)}, f32[16,4096]{1,0:T(8,128)S(1)}) custom-call(bf16[192,512]{1,0:T(8,128)(2,1)} %refs_0_.1, f32[1,512]{1,0:T(1,128)} %bitcast.2, bf16[512,4096]{1,0:T(8,128)(2,1)} %refs_2_.1, bf16[192,4096]{1,0:T(8,128)(2,1)} %refs_3_.1), custom_call_target="tpu_custom_call" | custom-call | tf_op jit(solution)/shard_map/pallas_call | solution.py:409
  30.7 0.8 %shard_map.68 = (bf16[192,512]{1,0:T(8,128)(2,1)}, f32[1,512]{1,0:T(1,128)}, f32[16,4096]{1,0:T(8,128)}) custom-call(bf16[192,512]{1,0:T(8,128)(2,1)S(1)} %get-tuple-element.9.first_in, f32[1,512]{1,0:T(1,128)S(1)} %get-tuple-element.10.second_in, f32[16,4096]{1,0:T(8,128)S(1)} %get-tuple-element.11.third_in), custom_call_target="tpu_custom_call" | custom-call | tf_op jit(solution)/shard_map/pallas_call | solution.py:384

commit v2 on v1

--- a/solution.py
+++ b/solution.py
@@ -9,22 +9,23 @@
 
 epsilon = 1e-06
 MESH = pl.DeviceIdType.MESH
-FIRST_Z = (2, 4)
-PAIRS = (2, 3, 2, 2, 2, 2)
+FIRST_Z = (2, 2, 2, 2)
+PAIRS = (2, 2, 4, 2, 2)
 GRANULES = 32
 SEND, PASS, SPREAD, FINISH, NORM, GAIN = range(6)
-NORMS = 3
+NORMS = 4
 ORDER = (
-    (SEND, 0), (SEND, 2), (SEND, 3), (SEND, 1), (SEND, 4), (SEND, 5),
-    (SEND, 6), (SEND, 7), (SEND, 8), (PASS, 2), (PASS, 3), (NORM, 0),
-    (NORM, 1), (SEND, 9), (SEND, 10), (NORM, 2), (SEND, 11), (SEND, 12),
-    (PASS, 4), (PASS, 5), (PASS, 0), (PASS, 6), (PASS, 7), (SPREAD, 2),
-    (PASS, 8), (GAIN, 0), (SPREAD, 3), (PASS, 9), (SEND, 13), (PASS, 10),
-    (PASS, 11), (PASS, 1), (SPREAD, 4), (PASS, 12), (FINISH, 2), (SPREAD, 6),
-    (FINISH, 3), (SPREAD, 5), (SPREAD, 8), (FINISH, 0), (SPREAD, 7), (GAIN, 1),
-    (SPREAD, 9), (PASS, 13), (FINISH, 4), (SPREAD, 11), (SPREAD, 10), (FINISH, 6),
-    (FINISH, 1), (SPREAD, 12), (SPREAD, 13), (FINISH, 5), (FINISH, 8), (FINISH, 7),
-    (FINISH, 9), (FINISH, 11), (GAIN, 2), (FINISH, 10), (FINISH, 12), (FINISH, 13),
+    (SEND, 1), (SEND, 13), (SEND, 4), (SEND, 10), (SEND, 7), (SEND, 6),
+    (SEND, 0), (SEND, 5), (PASS, 4), (PASS, 1), (SEND, 2), (PASS, 13),
+    (PASS, 7), (PASS, 10), (PASS, 0), (SEND, 11), (SEND, 12), (NORM, 0),
+    (SPREAD, 4), (SEND, 8), (PASS, 6), (SPREAD, 13), (PASS, 5), (SPREAD, 10),
+    (SEND, 9), (SEND, 3), (PASS, 2), (NORM, 1), (NORM, 2), (SPREAD, 6),
+    (PASS, 11), (SPREAD, 7), (PASS, 12), (NORM, 3), (PASS, 3), (PASS, 8),
+    (GAIN, 0), (FINISH, 10), (PASS, 9), (SPREAD, 5), (SPREAD, 2), (SPREAD, 1),
+    (FINISH, 13), (SPREAD, 12), (SPREAD, 11), (SPREAD, 0), (SPREAD, 9), (GAIN, 1),
+    (SPREAD, 8), (SPREAD, 3), (FINISH, 7), (FINISH, 1), (FINISH, 0), (FINISH, 6),
+    (FINISH, 11), (FINISH, 9), (FINISH, 3), (GAIN, 2), (FINISH, 4), (FINISH, 2),
+    (FINISH, 5), (FINISH, 12), (FINISH, 8),
 )
 
 
@@ -64,32 +65,45 @@
 
 
 def unit_list():
-    units, start = [], 0
-    for width in FIRST_Z:
-        units.append(("z", start, width))
-        start += width
-    for width in PAIRS:
-        for kind in ("x", "y"):
-            units.append((kind, start, width))
+    sizes = [("z", width) for width in FIRST_Z]
+    sizes += [(kind, width) for width in PAIRS for kind in ("x", "y")]
+    units, start = {}, 0
+    for stage, unit in ORDER:
+        if stage == SEND:
+            kind, width = sizes[unit]
+            units[unit] = (kind, start, width)
             start += width
-    return units
-
-
+    return [units[unit] for unit in range(len(sizes))]
+
+
+def share_list():
+    shares, start, end = [], 0, 0
+    for stage, unit in ORDER:
+        if stage == SEND:
+            end += UNITS[unit][2]
+            if len(shares) < 3 or end - start >= 6 or end == GRANULES:
+                shares.append((start, end))
+                start = end
+    return shares
+
+
+KINDS = ("z", "x", "y")
 UNITS = unit_list()
-
-
-def buffers(planes, kind, tokens, rows, width):
+SHARES = share_list()
+
+
+def buffers(planes, kind, rows, width):
     bf16, f32 = jnp.bfloat16, jnp.float32
-    shapes = [((tokens, width), bf16), ((tokens, width), bf16)]
     if kind == "z":
-        shapes += [
-            ((planes - 1, 4 * rows, width), bf16), ((planes - 1, 4 * rows, width), bf16),
-            ((4 * rows, width), f32),
+        shapes = [
+            ((3, 4 * rows, width), bf16), ((3, 4 * rows, width), bf16),
+            ((4, 4 * rows, width), f32),
+            ((2, 4 * rows, width), bf16), ((4 * rows, width), bf16),
             ((3, rows, width), bf16), ((3, rows, width), bf16), ((rows, width), f32),
         ]
     else:
         half, quarter = 2 * planes * rows, planes * rows
-        shapes += [
+        shapes = [
             ((half, width), bf16), ((half, width), bf16), ((half, width), f32),
             ((quarter, width), bf16), ((quarter, width), bf16), ((quarter, width), f32),
             ((planes - 1, rows, width), bf16), ((planes - 1, rows, width), bf16),
@@ -108,10 +122,10 @@
 
     latent_hbm, gain_hbm, weight_hbm, grad_hbm = take(4)
     latent_out, gain_out, weight_out = take(3)
-    latent_ref, gain_ref, weight, turned, peer_turned, left = take(6)
+    latent_ref, gain_ref, own_grad, peer_grad, weight, turned, peer_turned, left = take(8)
     grad_norm, gain_send, gain_pair, gain_quad, gain_line = take(5)
-    held = [take(8 if kind == "z" else 11) for kind, _, _ in UNITS]
-    small_sem, local_sem, grad_sem, one_sem, two_sem, three_sem, gain_sem = take(7)
+    held = [take(8 if kind == "z" else 9) for kind, _, _ in UNITS]
+    small_sem, load_sem, grad_sem, local_sem, one_sem, two_sem, three_sem, gain_sem = take(8)
 
     rows = weight_out.shape[0]
     me = lax.axis_index("dp")
@@ -121,6 +135,12 @@
     over_y = me + 4 - 8 * y
     over_xy = over_x + 4 - 8 * y
     lines = [((z + step) % planes) * 8 + me % 8 for step in range(1, planes)]
+    side = z // 2
+    inner = (z + side) % 2 == 1
+    near, far_inner, far_end = z + 1 - 2 * (z % 2), 2 - side, 3 - 3 * side
+    near_device, far_inner_device, far_end_device = [
+        plane * 8 + me % 8 for plane in (near, far_inner, far_end)
+    ]
     quad = [over_x, over_y, over_xy]
     peers = [partner] + quad + lines
 
@@ -140,13 +160,18 @@
     ]
     for copy in small_loads:
         copy.start()
-    firsts = [unit for stage, unit in ORDER if stage == SEND]
-    loads = {}
-    for unit in firsts:
-        loads[unit] = pltpu.make_async_copy(
-            grad_hbm.at[:, columns(unit)], held[unit][0], local_sem.at[unit]
+    loads = []
+    for at, (start, end) in enumerate(SHARES):
+        part = pl.ds(start * granule, (end - start) * granule)
+        loads.append(
+            pltpu.make_async_copy(grad_hbm.at[:, part], own_grad.at[:, part], load_sem.at[at])
         )
-        loads[unit].start()
+
+    def start_loads(chosen):
+        for copy in chosen:
+            copy.start()
+
+    start_loads(loads[:3])
 
     barrier = pltpu.get_barrier_semaphore()
     for peer in peers:
@@ -154,6 +179,7 @@
 
     for copy in small_loads:
         copy.wait()
+    start_loads(loads[3:])
     scaled_rows, _ = normalize(latent_ref[...])
     normed = scaled_rows * gain_ref[...]
     flipped = normed.T.astype(jnp.bfloat16)
@@ -167,23 +193,30 @@
         turned.at[1 - core], peer_turned, small_sem.at[0], small_sem.at[2], partner
     )
     turned_copy.start()
-    grads = {}
-
-    def share_grads(units):
-        for unit in units:
-            loads[unit].wait()
-            grads[unit] = send(
-                held[unit][0], held[unit][1], local_sem.at[unit], grad_sem.at[unit], partner
+    grads = []
+
+    def share_grads(upto):
+        for at in range(len(grads), upto):
+            loads[at].wait()
+            part = pl.ds(SHARES[at][0] * granule, (SHARES[at][1] - SHARES[at][0]) * granule)
+            grads.append(
+                send(
+                    own_grad.at[:, part], peer_grad.at[:, part],
+                    load_sem.at[at], grad_sem.at[at], partner,
+                )
             )
-            grads[unit].start()
-
-    share_grads(firsts[:1])
+            grads[at].start()
+
+    share_grads(1)
     weight_load = pltpu.make_async_copy(weight_hbm, weight, small_sem.at[1])
 
-    def block(step, away_y, away_x):
+    def block(plane, away_y, away_x):
         to_y = (1 - y) if away_y else y
         to_x = (1 - x) if away_x else x
-        return ((z + step) % planes) * 4 + to_y * 2 + to_x
+        return plane * 4 + to_y * 2 + to_x
+
+    by_role = (z, near, far_inner, far_end)
+    by_step = [(z + step) % planes for step in range(planes)]
 
     def arrange(kind, side, source):
         for step in range(planes):
@@ -191,41 +224,56 @@
                 for second in range(2):
                     if kind == "z":
                         place = step * 4 + first * 2 + second
-                        left[0, side, place] = source(block(step, first, second))
+                        left[0, side, place] = source(block(by_role[step], first, second))
                     else:
                         place = (first * 2 + second) * planes + step
                         if kind == "x":
-                            index = block(step, second == 0, first == 0)
+                            index = block(by_step[step], second == 0, first == 0)
                         else:
-                            index = block(step, first == 0, second == 0)
-                        left[1 if kind == "x" else 2, side, place] = source(index)
-
-    arrange("z", 0, lambda index: turned[core, index])
-    share_grads(firsts[1:3])
-    for kind in ("x", "y"):
+                            index = block(by_step[step], first == 0, second == 0)
+                        left[KINDS.index(kind), side, place] = source(index)
+
+    def left_of(unit, side):
+        which = KINDS.index(UNITS[unit][0])
+        return left[which, side].reshape(planes * 4 * rows, left.shape[-1])
+
+    def own_part(unit):
+        return jnp.dot(
+            left_of(unit, 0), own_grad[:, columns(unit)], preferred_element_type=jnp.float32
+        )
+
+    firsts = [unit for stage, unit in ORDER if stage == SEND]
+    kinds = []
+    for stage, unit in ORDER:
+        if stage == SEND and UNITS[unit][0] not in kinds:
+            kinds.append(UNITS[unit][0])
+    for count, kind in enumerate(kinds):
         arrange(kind, 0, lambda index: turned[core, index])
-    share_grads(firsts[3:])
+        if count == 0:
+            early = own_part(firsts[0])
+        share_grads(len(SHARES) if count == 2 else count + 2)
     weight_load.start()
     turned_copy.wait_recv()
+    arrived = set()
     arranged = set()
 
     half_rows = planes * 2 * rows
     quarter_rows = planes * rows
-    local, ones, twos, threes = dict(grads), {}, {}, {}
+    local, ones, twos, threes = {}, {}, {}, {}
 
     def partial_of(unit):
-        kind = UNITS[unit][0]
+        kind, start, _ = UNITS[unit]
+        for at, (first, end) in enumerate(SHARES):
+            if first <= start < end and at not in arrived:
+                grads[at].wait_recv()
+                arrived.add(at)
         if kind not in arranged:
             arrange(kind, 1, lambda index: peer_turned[index])
             arranged.add(kind)
-        which = ("z", "x", "y").index(kind)
-        sides = [
-            left[which, side].reshape(planes * 4 * rows, left.shape[-1]) for side in range(2)
-        ]
-        grads[unit].wait_recv()
-        return jnp.dot(
-            sides[0], held[unit][0][...], preferred_element_type=jnp.float32
-        ) + jnp.dot(sides[1], held[unit][1][...], preferred_element_type=jnp.float32)
+        own = early if unit == firsts[0] else own_part(unit)
+        return own + jnp.dot(
+            left_of(unit, 1), peer_grad[:, columns(unit)], preferred_element_type=jnp.float32
+        )
 
     def along_z(unit, source, target, recv_sem):
         for step, device in enumerate(lines):
@@ -234,18 +282,38 @@
             ).start()
         return send(source, target, local_sem.at[unit], recv_sem, lines[0])
 
+    def to_near(unit):
+        outgoing, incoming = held[unit][:2]
+        sems = (local_sem.at[unit], one_sem.at[unit], near_device)
+        return send(outgoing.at[0], incoming.at[0], *sems), send(outgoing, incoming, *sems)
+
+    def to_far(unit):
+        outgoing, incoming = held[unit][3:5]
+        sems = (local_sem.at[unit], two_sem.at[unit])
+        return (
+            send(outgoing.at[1], incoming, *sems, far_end_device),
+            send(outgoing.at[0], incoming, *sems, far_inner_device),
+        )
+
     def stage_send(unit):
         kind = UNITS[unit][0]
         partial = partial_of(unit)
-        local[unit].wait_send()
         if kind == "z":
-            outgoing, incoming, keep = held[unit][2:5]
+            outgoing, incoming, keep = held[unit][:3]
             split = partial.reshape(planes, 4 * rows, partial.shape[1])
             outgoing[...] = split[1:].astype(jnp.bfloat16)
-            keep[...] = split[0]
-            local[unit] = ones[unit] = along_z(unit, outgoing, incoming, one_sem.at[unit])
+            keep[...] = split
+            outward, inward = to_near(unit)
+
+            @pl.when(inner)
+            def _():
+                outward.start()
+
+            @pl.when(jnp.logical_not(inner))
+            def _():
+                inward.start()
         else:
-            outgoing, incoming, keep = held[unit][2:5]
+            outgoing, incoming, keep = held[unit][:3]
             outgoing[...] = partial[:half_rows].astype(jnp.bfloat16)
             keep[...] = partial[half_rows:]
             local[unit] = ones[unit] = send(
@@ -256,14 +324,50 @@
 
     def stage_pass(unit):
         kind = UNITS[unit][0]
-        ones[unit].wait_recv()
-        local[unit].wait_send()
-        incoming, keep = held[unit][3:5]
-        total = keep[...]
+        incoming, keep = held[unit][1:3]
         if kind == "z":
-            for step in range(planes - 1):
-                total = total + incoming[step].astype(jnp.float32)
-            outgoing, landing, rest = held[unit][5:8]
+            outward, inward = to_near(unit)
+            onward = held[unit][3]
+
+            @pl.when(inner)
+            def _():
+                inward.wait_recv()
+                outward.wait_send()
+                onward[...] = (keep[2:4] + incoming[1:3].astype(jnp.float32)).astype(jnp.bfloat16)
+                for copy in to_far(unit):
+                    copy.start()
+
+            @pl.when(jnp.logical_not(inner))
+            def _():
+                outward.wait_recv()
+                inward.wait_send()
+        else:
+            ones[unit].wait_recv()
+            local[unit].wait_send()
+            total = keep[...]
+            total = total + incoming[...].astype(jnp.float32)
+            outgoing, landing, rest = held[unit][3:6]
+            outgoing[...] = total[:quarter_rows].astype(jnp.bfloat16)
+            rest[...] = total[quarter_rows:]
+            local[unit] = twos[unit] = send(
+                outgoing, landing, local_sem.at[unit], two_sem.at[unit],
+                over_y if kind == "x" else over_x,
+            )
+            twos[unit].start()
+
+    def stage_spread(unit):
+        if UNITS[unit][0] == "z":
+            copies = to_far(unit)
+            copies[0].wait_recv()
+
+            @pl.when(inner)
+            def _():
+                for copy in copies:
+                    copy.wait_send()
+
+            first, keep = held[unit][1:3]
+            second, outgoing, landing, rest = held[unit][4:8]
+            total = keep[0] + first[0].astype(jnp.float32) + second[...].astype(jnp.float32)
             total = total.reshape(4, rows, total.shape[1])
             outgoing[...] = total[1:].astype(jnp.bfloat16)
             rest[...] = total[0]
@@ -275,21 +379,10 @@
             local[unit] = threes[unit] = send(
                 outgoing, landing, local_sem.at[unit], three_sem.at[unit], over_x
             )
-        else:
-            total = total + incoming[...].astype(jnp.float32)
-            outgoing, landing, rest = held[unit][5:8]
-            outgoing[...] = total[:quarter_rows].astype(jnp.bfloat16)
-            rest[...] = total[quarter_rows:]
-            local[unit] = twos[unit] = send(
-                outgoing, landing, local_sem.at[unit], two_sem.at[unit],
-                over_y if kind == "x" else over_x,
-            )
-            twos[unit].start()
-
-    def stage_spread(unit):
+            return
         twos[unit].wait_recv()
         local[unit].wait_send()
-        landing, keep, outgoing, incoming, rest = held[unit][6:11]
+        landing, keep, outgoing, incoming, rest = held[unit][4:9]
         total = keep[...] + landing[...].astype(jnp.float32)
         total = total.reshape(planes, rows, total.shape[1])
         outgoing[...] = total[1:].astype(jnp.bfloat16)
@@ -314,14 +407,13 @@
     def norm_piece(piece):
         if piece == 0:
             weight_load.wait()
-        share = -(-len(firsts) // NORMS)
-        total = None if piece == 0 else grad_norm[...]
-        for unit in firsts[piece * share : (piece + 1) * share]:
-            product = lax.dot_general(
-                held[unit][0][...], weight[:, columns(unit)], (((1,), (1,)), ((), ())),
-                preferred_element_type=jnp.float32,
-            )
-            total = product if total is None else total + product
+        part = pl.ds(piece * GRANULES // NORMS * granule, GRANULES // NORMS * granule)
+        total = lax.dot_general(
+            own_grad[:, part], weight[:, part], (((1,), (1,)), ((), ())),
+            preferred_element_type=jnp.float32,
+        )
+        if piece:
+            total = grad_norm[...] + total
         grad_norm[...] = total
         if piece == NORMS - 1:
             scaled, inverse = normalize(latent_ref[...])
@@ -365,7 +457,7 @@
         stages[stage](unit)
 
     turned_copy.wait_send()
-    for copy in local.values():
+    for copy in grads + list(local.values()):
         copy.wait_send()
 
 
@@ -405,7 +497,7 @@
     count = len(UNITS)
     held = []
     for kind, _, width in UNITS:
-        held += buffers(planes, kind, tokens, rows, width * granule)
+        held += buffers(planes, kind, rows, width * granule)
     latent_grad, gain_grad, weight_grad = pl.pallas_call(
         functools.partial(kernel, planes, factor, granule),
         out_shape=(
@@ -418,6 +510,8 @@
         scratch_shapes=[
             pltpu.VMEM((tokens, latent_width), bf16),
             pltpu.VMEM((1, latent_width), f32),
+            pltpu.VMEM((tokens, total_columns), bf16),
+            pltpu.VMEM((tokens, total_columns), bf16),
             pltpu.VMEM((latent_width, total_columns), bf16),
             pltpu.VMEM((2, planes * 4, rows, tokens), bf16),
             pltpu.VMEM((planes * 4, rows, tokens), bf16),
@@ -428,8 +522,8 @@
             pltpu.VMEM((3, 1, latent_width), f32),
             pltpu.VMEM((planes, 1, latent_width), f32),
             *held,
-            dma((3,)), dma((count,)), dma((count,)), dma((count,)),
-            dma((count,)), dma((count,)), dma((4,)),
+            dma((3,)), dma((len(SHARES),)), dma((len(SHARES),)), dma((count,)),
+            dma((count,)), dma((count,)), dma((count,)), dma((4,)),
         ],
         compiler_params=pltpu.CompilerParams(
             collective_id=0, has_side_effects=True, vmem_limit_bytes=67043328 - 512 * 1024
@@ -441,7 +535,7 @@
 
 def solution(mesh):
     devices = mesh.shape["dp"]
-    covered = mesh.shape["tensor"] == 1 and devices % 8 == 0 and 16 <= devices <= 32
+    covered = mesh.shape["tensor"] == 1 and devices == 32
     in_specs = (P("dp", None), P(), P(None, "tensor"), P("dp", "tensor"))
     out_specs = (P("dp", None), P(), P("dp", "tensor"))
     return jax.shard_map(

time: 31.6 us -> 30.7 us (0.972)
  Pallas kernels: 30.8 us -> 29.9 us
    pallas_call x1, Pallas kernels: 30 us -> 29.1 us  [fused(): pl.pallas_call(functools.partial(kernel, planes, factor, granule), out_sh...]
where the time goes in v2:
time: 30.7 us; the launch traced here: 30.5 us
  Pallas kernels  29.9 us (97%)
  between operations  0.64 us (2%)
    pallas_call x1, Pallas kernels, fused(): pl.pallas_call(functools.partial(kernel, planes, factor, granule), out_sh...  29.1 us
    pallas_call x1, Pallas kernels, place(): pl.pallas_call(place_kernel, out_shape=tuple((jax.ShapeDtypeStruct(a.shap...  0.8 us

profile of v2, /device:TPU:0, one launch (start us, length us, event | category | flops | bytes accessed | tf_op | source)
XLA Modules:
  0.0 30.5 jit_solution(2187138163398814303)
XLA Ops:
  0.6 29.1 %shard_map.67 = (bf16[192,512]{1,0:T(8,128)(2,1)S(1)}, f32[1,512]{1,0:T(1,128)S(1)}, f32[16,4096]{1,0:T(8,128)S(1)}) custom-call(bf16[192,512]{1,0:T(8,128)(2,1)} %refs_0_.1, f32[1,512]{1,0:T(1,128)} %bitcast.2, bf16[512,4096]{1,0:T(8,128)(2,1)} %refs_2_.1, bf16[192,4096]{1,0:T(8,128)(2,1)} %refs_3_.1), custom_call_target="tpu_custom_call" | custom-call | tf_op jit(solution)/shard_map/pallas_call | solution.py:501
  29.7 0.8 %shard_map.68 = (bf16[192,512]{1,0:T(8,128)(2,1)}, f32[1,512]{1,0:T(1,128)}, f32[16,4096]{1,0:T(8,128)}) custom-call(bf16[192,512]{1,0:T(8,128)(2,1)S(1)} %get-tuple-element.9.first_in, f32[1,512]{1,0:T(1,128)S(1)} %get-tuple-element.10.second_in, f32[16,4096]{1,0:T(8,128)S(1)} %get-tuple-element.11.third_in), custom_call_target="tpu_custom_call" | custom-call | tf_op jit(solution)/shard_map/pallas_call | solution.py:476
